TPU v7x, 32 devices: a whole 2x2x4 slice. The times are simulated.
32 devices in a mesh: rep: 4 (over y, x), fsdp: 8 (over z, core).
Axes of the slice: x: 2, y: 2, z: 4, core: 2. Of those that a mesh axis runs over, the one named last changes fastest.
Arguments:
- momentum: float32 [4, 18432, 2304], P('rep', 'fsdp'), may hold values from -60 to 60
- gradient: bfloat16 [4, 18432, 2304], P('rep', 'fsdp'), may hold values from -30 to 30
- right_factor: float32 [2304, 256], P('fsdp'), may hold values from -0.125 to 0.125
Outputs:
- new_momentum: float32 [4, 18432, 2304], P('rep', 'fsdp')
- update: bfloat16 [18432, 2304], P('fsdp')
- new_factor: float32 [2304, 256], P('fsdp')
All inputs are finite; a program needn't handle non-finite values.
Results may differ from a plain program's by a relative error of at most 0.001.
Values sent between devices are 32-bit elements; how exact they have to be, the bound alone decides.
A program may use at most 128 MiB of HBM per device.

v0:
```python
import math
import jax
import jax.numpy as jnp
from jax import lax
from jax.sharding import PartitionSpec as P

ROWS = 18432
COLS = 2304
RANK = 256
epsilon = 1e-06
decay_rate = 0.95
highest = lax.Precision.HIGHEST


def shards(momentum, gradient, right_factor):
    buffer = momentum[0] + gradient[0].astype(jnp.float32)
    replicas = lax.axis_size("rep")
    columns = buffer
    partial_left = jnp.dot(
        columns,
        lax.all_gather(right_factor, "fsdp", axis=0, tiled=True),
        precision=highest,
        preferred_element_type=jnp.float32,
    )
    projected = lax.psum(partial_left, "rep")
    local_gram = jnp.dot(
        projected.T, projected, precision=highest, preferred_element_type=jnp.float32
    )
    gram_matrix = lax.psum(local_gram, "fsdp")
    lower_factor = jnp.linalg.cholesky(gram_matrix)
    orthonormal = jax.scipy.linalg.solve_triangular(lower_factor, projected.T, lower=True).T
    columns = buffer
    scattered = lax.psum_scatter(
        lax.dot_general(
            columns,
            orthonormal,
            (((0,), (0,)), ((), ())),
            precision=highest,
            preferred_element_type=jnp.float32,
        ),
        "fsdp",
        scatter_dimension=0,
        tiled=True,
    )
    own_factor = lax.psum(scattered, "rep") / replicas
    full_factor = lax.all_gather(own_factor, "fsdp", axis=0, tiled=True)
    col_norms = jnp.sqrt(jnp.sum(full_factor * full_factor, axis=0) + epsilon)
    new_factor = own_factor / col_norms
    correction = lax.dot_general(
        orthonormal,
        full_factor,
        (((1,), (1,)), ((), ())),
        precision=highest,
        preferred_element_type=jnp.float32,
    )
    new_momentum = (buffer - (1.0 - decay_rate) * correction)[None]
    direction = lax.dot_general(
        orthonormal,
        full_factor / col_norms,
        (((1,), (1,)), ((), ())),
        precision=highest,
        preferred_element_type=jnp.float32,
    )
    update = (math.sqrt(ROWS * COLS / RANK) * direction).astype(jnp.bfloat16)
    return (new_momentum, update, new_factor)


def solution(mesh):
    in_specs = (P("rep", "fsdp", None), P("rep", "fsdp", None), P("fsdp", None))
    out_specs = (P("rep", "fsdp", None), P("fsdp", None), P("fsdp", None))
    return jax.shard_map(shards, mesh=mesh, in_specs=in_specs, out_specs=out_specs, check_vma=False)
```

profile of v0, /device:TPU:0, one launch (start us, length us, event | category | flops | bytes accessed | tf_op | source)
XLA Modules:
  0.0 512.4 jit_solution(980822565762107197)
XLA Ops:
  7.2 0.0 all-gather.3.cloned.1.call-start
  7.2 0.7 all-gather.3.cloned.1.call-update
  7.9 0.0 all-reduce.5.cloned.1.call-start
  7.9 35.9 %all-gather.3.cloned.1.call-done = f32[2304,256]{1,0:T(8,128)} async-done(((f32[288,256]{1,0:T(8,128)}), f32[2304,256]{1,0:T(8,128)}) %all-gather.3.cloned.1.call-update) | async-done | bytes 2359312 | tf_op jit(solution)/shard_map/all_gather | solution.py:21
  43.8 22.8 %fusion.3 = f32[2304,256]{1,0:T(8,128)} fusion(f32[2304,256]{1,0:T(8,128)} %all-gather.3.cloned.1.call-done, f32[1,2304,2304]{2,1,0:T(8,128)} %param.3, bf16[1,2304,2304]{2,1,0:T(8,128)(2,1)} %param.4), kind=kOutput, calls=%fused_computation.7 | convolution fusion | flops 16318070784 | bytes 36569088 | tf_op jit(solution)/shard_map/dot_general | solution.py:19
  66.6 0.0 all-reduce.5.cloned.1.call-update
  66.6 0.0 all-reduce.7.cloned.1.call-start
  66.7 73.2 %all-reduce.5.cloned.1.call-done = f32[2304,256]{1,0:T(8,128)} async-done(((f32[2304,256]{1,0:T(8,128)}), f32[2304,256]{1,0:T(8,128)}) %all-reduce.5.cloned.1.call-update) | async-done | bytes 2359312 | tf_op jit(solution)/shard_map/psum | solution.py:25
  139.9 6.9 %fusion.21 = f32[256,256]{0,1:T(8,128)} fusion(f32[2304,256]{1,0:T(8,128)} %all-reduce.5.cloned.1.call-done), kind=kOutput, calls=%fused_computation.48 | convolution fusion | flops 1811939328 | bytes 2621440 | tf_op jit(solution)/shard_map/dot_general | solution.py:26
  146.8 0.0 all-reduce.7.cloned.1.call-update
  146.9 0.3 reduce-scatter.2.cloned.1.call-start
  147.1 55.3 %all-reduce.7.cloned.1.call-done = f32[256,256]{0,1:T(8,128)} async-done(((f32[256,256]{0,1:T(8,128)}), f32[256,256]{0,1:T(8,128)}) %all-reduce.7.cloned.1.call-update) | async-done | bytes 262160 | tf_op jit(solution)/shard_map/psum | solution.py:29
  202.4 1.1 copy.7
  203.5 1.0 fusion.11
  204.5 11.7 %cholesky.50 = f32[128,128]{1,0:T(8,128)S(1)} custom-call(f32[128,128]{1,0:T(8,128)S(1)} %cholesky.118), custom_call_target="Cholesky" | custom-call | tf_op jit(solution)/shard_map/jit(cholesky)/cholesky | solution.py:30
  216.3 9.8 %custom-call.15 = f32[1,128,128]{1,2,0:T(8,128)S(1)} custom-call(f32[1,128,128]{2,1,0:T(8,128)S(1)} %get-tuple-element.24), custom_call_target="InvertDiagBlocksLowerTriangular" | custom-call | tf_op jit(solution)/shard_map/jit(cholesky)/cholesky | solution.py:30
  226.1 0.2 constant_dynamic-update-slice_fusion.1
  226.3 0.3 convolution_subtract_fusion.1
  226.6 11.7 %cholesky.105 = f32[128,128]{1,0:T(8,128)S(1)} custom-call(f32[128,128]{1,0:T(8,128)S(1)} %convolution_subtract_fusion.1), custom_call_target="Cholesky" | custom-call | tf_op jit(solution)/shard_map/jit(cholesky)/cholesky | solution.py:30
  238.3 0.6 compare_reduce_fusion
  240.3 0.1 triangular_solve.57
  240.4 4.4 while.1
  240.8 0.6 fusion.31
  241.4 1.4 bitcast_dynamic-update-slice_fusion.2
  242.8 0.6 fusion.31
  243.4 1.4 bitcast_dynamic-update-slice_fusion.2
  244.8 0.0 copy-start.1
  244.8 20.3 %custom-call.16 = f32[2,128,128]{1,2,0:T(8,128)} custom-call(f32[2,128,128]{2,1,0:T(8,128)S(1)} %get-tuple-element.10), custom_call_target="InvertDiagBlocksLowerTriangular" | custom-call | tf_op jit(solution)/shard_map/jit(_solve_triangular)/triangular_solve | solution.py:31
  265.1 2.0 fusion.8
  267.1 0.0 copy-start.3
  267.1 2.9 convolution_subtract_fusion
  270.0 1.2 fusion.13
  271.2 38.5 %fusion.1 = f32[2304,256]{1,0:T(8,128)} fusion(f32[1,2304,2304]{2,1,0:T(8,128)} %param.3, bf16[1,2304,2304]{2,1,0:T(8,128)(2,1)} %param.4, f32[128,2304]{1,0:T(8,128)S(1)} %fusion.13, f32[128,2304]{1,0:T(8,128)S(1)} %fusion.8), kind=kOutput, calls=%fused_computation.5 | convolution fusion | flops 16318660608 | bytes 36569088 | tf_op jit(solution)/shard_map/dot_general | solution.py:34
  309.7 0.0 reduce-scatter.2.cloned.1.call-update
  309.7 0.0 all-reduce.9.cloned.1.call-start
  309.7 36.2 %reduce-scatter.2.cloned.1.call-done = f32[288,256]{1,0:T(8,128)} async-done(((f32[2304,256]{1,0:T(8,128)}), f32[288,256]{1,0:T(8,128)}) %reduce-scatter.2.cloned.1.call-update) | async-done | bytes 294928 | tf_op jit(solution)/shard_map/reduce_scatter | solution.py:33
  345.9 0.0 all-reduce.9.cloned.1.call-update
  346.0 0.0 all-gather.5.cloned.1.call-start
  346.0 45.0 %all-reduce.9.cloned.1.call-done = f32[288,256]{1,0:T(8,128)} async-done(((f32[288,256]{1,0:T(8,128)}), f32[288,256]{1,0:T(8,128)}) %all-reduce.9.cloned.1.call-update) | async-done | bytes 294928 | tf_op jit(solution)/shard_map/psum | solution.py:45
  391.0 1.8 broadcast_multiply_fusion
  392.8 0.0 all-gather.5.cloned.1.call-update
  392.8 31.8 %all-gather.5.cloned.1.call-done = f32[2304,256]{1,0:T(8,128)} async-done(((f32[288,256]{1,0:T(8,128)}), f32[2304,256]{1,0:T(8,128)}) %all-gather.5.cloned.1.call-update) | async-done | bytes 2359312 | tf_op jit(solution)/shard_map/all_gather | solution.py:46
  424.5 2.1 multiply_reduce_fusion
  426.7 0.0 copy-done.2
  426.7 0.7 broadcast_divide_fusion
  427.4 36.8 %fusion.6 = bf16[2304,2304]{1,0:T(8,128)(2,1)} fusion(f32[2304,256]{1,0:T(8,128)} %all-gather.5.cloned.1.call-done, f32[128,2304]{1,0:T(8,128)S(1)} %fusion.13, f32[128,2304]{1,0:T(8,128)S(1)} %fusion.8, f32[256]{0:T(256)S(1)} %add_sqrt_fusion), kind=kOutput, calls=%fused_computation.11 | convolution fusion | flops 16319250432 | bytes 15336448 | tf_op jit(solution)/shard_map/dot_general | solution.py:57
  464.3 0.0 slice-done
  464.3 40.8 %fusion.5 = f32[1,2304,2304]{2,1,0:T(8,128)} fusion(f32[2304,256]{1,0:T(8,128)} %all-gather.5.cloned.1.call-done, f32[1,2304,2304]{2,1,0:T(8,128)} %param.3, bf16[1,2304,2304]{2,1,0:T(8,128)(2,1)S(1)} %bitcast.47, f32[128,2304]{1,0:T(8,128)S(1)} %fusion.13, f32[128,2304]{1,0:T(8,128)S(1)} %fusion.8), kind=kOutput, calls=%fused_computation.10 | convolution fusion | flops 16329277440 | bytes 57802752 | tf_op jit(solution)/shard_map/dot_general | solution.py:49
  (21 shorter events, 0.2 us)
Async XLA Ops:
  7.2 36.6 %all-gather.3.cloned.1.call-start = ((), (), s32[]{:S(2)}) async-start(), calls=%async_computation.1 | async-start | bytes 2654208 | tf_op jit(solution)/shard_map/all_gather | solution.py:21
  7.9 132.0 %all-reduce.5.cloned.1.call-start = ((), (), s32[]{:S(2)}) async-start(), calls=%async_computation.2 | async-start | bytes 4718592 | tf_op jit(solution)/shard_map/psum | solution.py:25
  66.6 135.8 %all-reduce.7.cloned.1.call-start = ((), (), s32[]{:S(2)}) async-start(), calls=%async_computation.3 | async-start | bytes 524288 | tf_op jit(solution)/shard_map/psum | solution.py:29
  146.8 118.3 %copy-start = (f32[2304,256]{1,0:T(8,128)S(1)}, f32[2304,256]{1,0:T(8,128)}, u32[]{:S(2)}) copy-start(f32[2304,256]{1,0:T(8,128)} %all-reduce.5.cloned.1.call-done) | copy-start | bytes 7077892
  146.9 199.1 %reduce-scatter.2.cloned.1.call-start = ((), (), s32[]{:S(2)}) async-start(), calls=%async_computation.4 | async-start | bytes 2654208 | tf_op jit(solution)/shard_map/reduce_scatter | solution.py:33
  244.8 20.3 %copy-start.1 = (f32[256,256]{1,0:T(8,128)}, f32[256,256]{1,0:T(8,128)S(1)}, u32[]{:S(2)}) copy-start(f32[256,256]{1,0:T(8,128)S(1)} %get-tuple-element.86) | copy-start | bytes 786436
  267.1 2.9 copy-start.3
  309.7 81.3 %all-reduce.9.cloned.1.call-start = ((), (), s32[]{:S(2)}) async-start(), calls=%async_computation.5 | async-start | bytes 589824 | tf_op jit(solution)/shard_map/psum | solution.py:45
  346.0 78.6 %all-gather.5.cloned.1.call-start = ((), (), s32[]{:S(2)}) async-start(), calls=%async_computation.6 | async-start | bytes 2654208 | tf_op jit(solution)/shard_map/all_gather | solution.py:46
  391.0 35.7 %copy-start.2 = (f32[288,256]{1,0:T(8,128)S(1)}, f32[288,256]{1,0:T(8,128)}, u32[]{:S(2)}) copy-start(f32[288,256]{1,0:T(8,128)} %all-reduce.9.cloned.1.call-done) | copy-start | bytes 884740
  424.5 39.7 %slice-start = ((s8[10616832]{0:T(1024)(128)(4,1)}), s8[4194304]{0:T(1024)(128)(4,1)S(1)}, s32[]{:S(2)}) async-start(s8[10616832]{0:T(1024)(128)(4,1)} %bitcast.46), calls=%async_computation.7 | async-start | bytes 8388608
  427.4 36.8 %slice-start.1 = ((s8[10616832]{0:T(1024)(128)(4,1)}), s8[4194304]{0:T(1024)(128)(4,1)S(1)}, s32[]{:S(2)}) async-start(s8[10616832]{0:T(1024)(128)(4,1)} %bitcast.46), calls=%async_computation.8 | async-start | bytes 8388608
  427.4 36.8 %slice-start.2 = ((s8[10616832]{0:T(1024)(128)(4,1)}), s8[2228224]{0:T(1024)(128)(4,1)S(1)}, s32[]{:S(2)}) async-start(s8[10616832]{0:T(1024)(128)(4,1)} %bitcast.46), calls=%async_computation.9 | async-start | bytes 4456448
Sparse Core Ops, SparseCore 0:
  9.6 34.1 all-gather.2
  66.8 73.0 all-reduce.4
  147.0 55.4 all-reduce.6
  309.8 36.0 reduce-scatter.1
  348.7 42.2 all-reduce.8
  393.1 31.4 all-gather.4
where the time goes:
time: 520 us; the launch traced here: 512 us
  waiting for transfers between devices  278 us (53%)
  matrix products  152 us (29%)
  other arithmetic  59.9 us (12%)
  between operations  16 us (3%)
    psum x1, waiting for transfers between devices, shards(): projected = lax.psum(partial_left, 'rep')  73.2 us
    psum x1, waiting for transfers between devices, shards(): gram_matrix = lax.psum(local_gram, 'fsdp')  55.3 us
    psum x1, waiting for transfers between devices, shards(): own_factor = lax.psum(scattered, 'rep') / replicas  45 us
    dot_general x1, matrix products, shards(): lax.dot_general(orthonormal, full_factor, (((1,), (1,)), ((), ())), preci...  40.8 us
    dot_general x1, matrix products, shards(): lax.dot_general(columns, orthonormal, (((0,), (0,)), ((), ())), precision...  38.5 us
    dot_general x1, matrix products, shards(): lax.dot_general(orthonormal, full_factor / col_norms, (((1,), (1,)), ((),...  36.8 us
    reduce_scatter x1, waiting for transfers between devices, shards(): lax.psum_scatter(lax.dot_general(columns, orthonormal, (((0,), (0,)), (()...  36.2 us
    all_gather x1, waiting for transfers between devices, shards(): lax.all_gather(right_factor, 'fsdp', axis=0, tiled=True)  35.9 us
  transfers between devices with their start and end apart: 6, of which 6 were waited for; matrix products, arithmetic and copies ran while one was open for 0% of the time, Pallas kernels for 0%

commit v1 on v0

--- a/solution.py
+++ b/solution.py
@@ -10,6 +10,11 @@
 epsilon = 1e-06
 decay_rate = 0.95
 highest = lax.Precision.HIGHEST
+
+
+def gather_and_add(x, axis):
+    terms = lax.all_gather(x, axis)
+    return jnp.sum(terms, axis=0)
 
 
 def shards(momentum, gradient, right_factor):
@@ -26,7 +31,7 @@
     local_gram = jnp.dot(
         projected.T, projected, precision=highest, preferred_element_type=jnp.float32
     )
-    gram_matrix = lax.psum(local_gram, "fsdp")
+    gram_matrix = gather_and_add(local_gram, "fsdp")
     lower_factor = jnp.linalg.cholesky(gram_matrix)
     orthonormal = jax.scipy.linalg.solve_triangular(lower_factor, projected.T, lower=True).T
     columns = buffer

time: 520 us -> 494 us (0.950)
  waiting for transfers between devices: 278 us -> 252 us
    psum x1 -> x0, waiting for transfers between devices: 55.3 us -> none  [shards(): gram_matrix = lax.psum(local_gram, 'fsdp')]
    all_gather x0 -> x1, waiting for transfers between devices: none -> 29 us  [gather_and_add(): terms = lax.all_gather(x, axis)]
where the time goes in v1:
time: 494 us; the launch traced here: 486 us
  waiting for transfers between devices  252 us (51%)
  matrix products  152 us (31%)
  other arithmetic  60.7 us (12%)
  between operations  16 us (3%)
    psum x1, waiting for transfers between devices, shards(): projected = lax.psum(partial_left, 'rep')  73.2 us
    psum x1, waiting for transfers between devices, shards(): own_factor = lax.psum(scattered, 'rep') / replicas  45 us
    dot_general x1, matrix products, shards(): lax.dot_general(orthonormal, full_factor, (((1,), (1,)), ((), ())), preci...  40.8 us
    dot_general x1, matrix products, shards(): lax.dot_general(columns, orthonormal, (((0,), (0,)), ((), ())), precision...  38.5 us
    dot_general x1, matrix products, shards(): lax.dot_general(orthonormal, full_factor / col_norms, (((1,), (1,)), ((),...  36.8 us
    reduce_scatter x1, waiting for transfers between devices, shards(): lax.psum_scatter(lax.dot_general(columns, orthonormal, (((0,), (0,)), (()...  36.6 us
    all_gather x1, waiting for transfers between devices, shards(): lax.all_gather(right_factor, 'fsdp', axis=0, tiled=True)  35.9 us
    another operation x6, other arithmetic, shards(): lower_factor = jnp.linalg.cholesky(gram_matrix)  33.9 us
  transfers between devices with their start and end apart: 6, of which 6 were waited for; matrix products, arithmetic and copies ran while one was open for 0% of the time, Pallas kernels for 0%

profile of v1, /device:TPU:0, one launch (start us, length us, event | category | flops | bytes accessed | tf_op | source)
XLA Modules:
  0.0 486.4 jit_solution(8685304740107629261)
XLA Ops:
  7.2 0.0 all-gather.5.cloned.1.call-start
  7.2 0.7 all-gather.5.cloned.1.call-update
  7.9 0.0 all-reduce.4.cloned.1.call-start
  7.9 35.9 %all-gather.5.cloned.1.call-done = f32[2304,256]{1,0:T(8,128)} async-done(((f32[288,256]{1,0:T(8,128)}), f32[2304,256]{1,0:T(8,128)}) %all-gather.5.cloned.1.call-update) | async-done | bytes 2359312 | tf_op jit(solution)/shard_map/all_gather | solution.py:26
  43.8 22.8 %fusion.3 = f32[2304,256]{1,0:T(8,128)} fusion(f32[2304,256]{1,0:T(8,128)} %all-gather.5.cloned.1.call-done, f32[1,2304,2304]{2,1,0:T(8,128)} %param.3, bf16[1,2304,2304]{2,1,0:T(8,128)(2,1)} %param.4), kind=kOutput, calls=%fused_computation.7 | convolution fusion | flops 16318070784 | bytes 36569088 | tf_op jit(solution)/shard_map/dot_general | solution.py:24
  66.6 0.0 all-reduce.4.cloned.1.call-update
  66.6 0.0 all-gather.9.cloned.1.call-start
  66.7 73.2 %all-reduce.4.cloned.1.call-done = f32[2304,256]{1,0:T(8,128)} async-done(((f32[2304,256]{1,0:T(8,128)}), f32[2304,256]{1,0:T(8,128)}) %all-reduce.4.cloned.1.call-update) | async-done | bytes 2359312 | tf_op jit(solution)/shard_map/psum | solution.py:30
  139.9 7.0 %fusion.21 = f32[256,256]{1,0:T(8,128)} fusion(f32[2304,256]{1,0:T(8,128)} %all-reduce.4.cloned.1.call-done), kind=kOutput, calls=%fused_computation.48 | convolution fusion | flops 1811939328 | bytes 2621440 | tf_op jit(solution)/shard_map/dot_general | solution.py:31
  146.9 0.0 all-gather.9.cloned.1.call-update
  146.9 0.3 reduce-scatter.2.cloned.1.call-start
  147.2 29.0 %all-gather.9.cloned.1.call-done = f32[2048,256]{1,0:T(8,128)} async-done(((f32[256,256]{1,0:T(8,128)}), f32[2048,256]{1,0:T(8,128)}) %all-gather.9.cloned.1.call-update) | async-done | bytes 2097168 | tf_op jit(solution)/shard_map/all_gather | solution.py:16
  176.2 1.8 reduce_sum.18
  177.9 0.0 copy-start
  177.9 0.1 copy.7
  178.1 11.7 %cholesky.50 = f32[128,128]{1,0:T(8,128)S(1)} custom-call(f32[128,128]{1,0:T(8,128)S(1)} %cholesky.118), custom_call_target="Cholesky" | custom-call | tf_op jit(solution)/shard_map/jit(cholesky)/cholesky | solution.py:35
  189.9 9.8 %custom-call.15 = f32[1,128,128]{1,2,0:T(8,128)S(1)} custom-call(f32[1,128,128]{2,1,0:T(8,128)S(1)} %get-tuple-element.24), custom_call_target="InvertDiagBlocksLowerTriangular" | custom-call | tf_op jit(solution)/shard_map/jit(cholesky)/cholesky | solution.py:35
  199.7 0.2 constant_dynamic-update-slice_fusion.1
  199.9 0.3 convolution_subtract_fusion.1
  200.2 11.7 %cholesky.105 = f32[128,128]{1,0:T(8,128)S(1)} custom-call(f32[128,128]{1,0:T(8,128)S(1)} %convolution_subtract_fusion.1), custom_call_target="Cholesky" | custom-call | tf_op jit(solution)/shard_map/jit(cholesky)/cholesky | solution.py:35
  212.0 0.6 compare_reduce_fusion
  213.9 0.1 triangular_solve.57
  214.0 4.4 while.1
  214.4 0.6 fusion.31
  215.0 1.4 bitcast_dynamic-update-slice_fusion.2
  216.4 0.6 fusion.31
  217.0 1.4 bitcast_dynamic-update-slice_fusion.2
  218.4 0.0 copy-start.1
  218.4 20.3 %custom-call.16 = f32[2,128,128]{1,2,0:T(8,128)} custom-call(f32[2,128,128]{2,1,0:T(8,128)S(1)} %get-tuple-element.10), custom_call_target="InvertDiagBlocksLowerTriangular" | custom-call | tf_op jit(solution)/shard_map/jit(_solve_triangular)/triangular_solve | solution.py:36
  238.7 2.0 fusion.8
  240.7 0.0 copy-start.3
  240.8 2.9 convolution_subtract_fusion
  243.7 1.2 fusion.13
  244.8 38.5 %fusion.1 = f32[2304,256]{1,0:T(8,128)} fusion(f32[1,2304,2304]{2,1,0:T(8,128)} %param.3, bf16[1,2304,2304]{2,1,0:T(8,128)(2,1)} %param.4, f32[128,2304]{1,0:T(8,128)S(1)} %fusion.13, f32[128,2304]{1,0:T(8,128)S(1)} %fusion.8), kind=kOutput, calls=%fused_computation.5 | convolution fusion | flops 16318660608 | bytes 36569088 | tf_op jit(solution)/shard_map/dot_general | solution.py:39
  283.3 0.0 reduce-scatter.2.cloned.1.call-update
  283.3 0.0 all-reduce.6.cloned.1.call-start
  283.4 36.6 %reduce-scatter.2.cloned.1.call-done = f32[288,256]{1,0:T(8,128)} async-done(((f32[2304,256]{1,0:T(8,128)}), f32[288,256]{1,0:T(8,128)}) %reduce-scatter.2.cloned.1.call-update) | async-done | bytes 294928 | tf_op jit(solution)/shard_map/reduce_scatter | solution.py:38
  319.9 0.0 all-reduce.6.cloned.1.call-update
  320.0 0.0 all-gather.7.cloned.1.call-start
  320.0 45.0 %all-reduce.6.cloned.1.call-done = f32[288,256]{1,0:T(8,128)} async-done(((f32[288,256]{1,0:T(8,128)}), f32[288,256]{1,0:T(8,128)}) %all-reduce.6.cloned.1.call-update) | async-done | bytes 294928 | tf_op jit(solution)/shard_map/psum | solution.py:50
  365.0 1.8 broadcast_multiply_fusion
  366.8 0.0 all-gather.7.cloned.1.call-update
  366.8 31.8 %all-gather.7.cloned.1.call-done = f32[2304,256]{1,0:T(8,128)} async-done(((f32[288,256]{1,0:T(8,128)}), f32[2304,256]{1,0:T(8,128)}) %all-gather.7.cloned.1.call-update) | async-done | bytes 2359312 | tf_op jit(solution)/shard_map/all_gather | solution.py:51
  398.6 2.1 multiply_reduce_fusion
  400.7 0.7 broadcast_divide_fusion
  401.5 36.8 %fusion.6 = bf16[2304,2304]{1,0:T(8,128)(2,1)} fusion(f32[2304,256]{1,0:T(8,128)} %all-gather.7.cloned.1.call-done, f32[128,2304]{1,0:T(8,128)S(1)} %fusion.13, f32[128,2304]{1,0:T(8,128)S(1)} %fusion.8, f32[256]{0:T(256)S(1)} %add_sqrt_fusion), kind=kOutput, calls=%fused_computation.11 | convolution fusion | flops 16319250432 | bytes 15336448 | tf_op jit(solution)/shard_map/dot_general | solution.py:62
  438.3 0.0 slice-done.2
  438.3 40.8 %fusion.5 = f32[1,2304,2304]{2,1,0:T(8,128)} fusion(f32[2304,256]{1,0:T(8,128)} %all-gather.7.cloned.1.call-done, f32[1,2304,2304]{2,1,0:T(8,128)} %param.3, bf16[1,2304,2304]{2,1,0:T(8,128)(2,1)S(1)} %bitcast.48, f32[128,2304]{1,0:T(8,128)S(1)} %fusion.13, f32[128,2304]{1,0:T(8,128)S(1)} %fusion.8), kind=kOutput, calls=%fused_computation.10 | convolution fusion | flops 16329277440 | bytes 57802752 | tf_op jit(solution)/shard_map/dot_general | solution.py:54
  (22 shorter events, 0.2 us)
Async XLA Ops:
  7.2 36.6 %all-gather.5.cloned.1.call-start = ((), (), s32[]{:S(2)}) async-start(), calls=%async_computation.1 | async-start | bytes 2654208 | tf_op jit(solution)/shard_map/all_gather | solution.py:26
  7.9 132.0 %all-reduce.4.cloned.1.call-start = ((), (), s32[]{:S(2)}) async-start(), calls=%async_computation.2 | async-start | bytes 4718592 | tf_op jit(solution)/shard_map/psum | solution.py:30
  66.6 109.5 %all-gather.9.cloned.1.call-start = ((), (), s32[]{:S(2)}) async-start(), calls=%async_computation.6 | async-start | bytes 2359296 | tf_op jit(solution)/shard_map/all_gather | solution.py:16
  146.9 173.1 %reduce-scatter.2.cloned.1.call-start = ((), (), s32[]{:S(2)}) async-start(), calls=%async_computation.3 | async-start | bytes 2654208 | tf_op jit(solution)/shard_map/reduce_scatter | solution.py:38
  177.9 60.8 %copy-start = (f32[2304,256]{1,0:T(8,128)S(1)}, f32[2304,256]{1,0:T(8,128)}, u32[]{:S(2)}) copy-start(f32[2304,256]{1,0:T(8,128)} %all-reduce.4.cloned.1.call-done) | copy-start | bytes 7077892
  218.4 20.3 %copy-start.1 = (f32[256,256]{1,0:T(8,128)}, f32[256,256]{1,0:T(8,128)S(1)}, u32[]{:S(2)}) copy-start(f32[256,256]{1,0:T(8,128)S(1)} %get-tuple-element.87) | copy-start | bytes 786436
  240.7 2.9 copy-start.3
  283.3 81.7 %all-reduce.6.cloned.1.call-start = ((), (), s32[]{:S(2)}) async-start(), calls=%async_computation.4 | async-start | bytes 589824 | tf_op jit(solution)/shard_map/psum | solution.py:50
  320.0 78.6 %all-gather.7.cloned.1.call-start = ((), (), s32[]{:S(2)}) async-start(), calls=%async_computation.5 | async-start | bytes 2654208 | tf_op jit(solution)/shard_map/all_gather | solution.py:51
  365.0 35.7 %copy-start.2 = (f32[288,256]{1,0:T(8,128)S(1)}, f32[288,256]{1,0:T(8,128)}, u32[]{:S(2)}) copy-start(f32[288,256]{1,0:T(8,128)} %all-reduce.6.cloned.1.call-done) | copy-start | bytes 884740
  398.6 39.7 %slice-start = ((s8[10616832]{0:T(1024)(128)(4,1)}), s8[4194304]{0:T(1024)(128)(4,1)S(1)}, s32[]{:S(2)}) async-start(s8[10616832]{0:T(1024)(128)(4,1)} %bitcast.47), calls=%async_computation.7 | async-start | bytes 8388608
  401.5 36.8 %slice-start.1 = ((s8[10616832]{0:T(1024)(128)(4,1)}), s8[4194304]{0:T(1024)(128)(4,1)S(1)}, s32[]{:S(2)}) async-start(s8[10616832]{0:T(1024)(128)(4,1)} %bitcast.47), calls=%async_computation.8 | async-start | bytes 8388608
  401.5 36.8 %slice-start.2 = ((s8[10616832]{0:T(1024)(128)(4,1)}), s8[2228224]{0:T(1024)(128)(4,1)S(1)}, s32[]{:S(2)}) async-start(s8[10616832]{0:T(1024)(128)(4,1)} %bitcast.47), calls=%async_computation.9 | async-start | bytes 4456448
Sparse Core Ops, SparseCore 0:
  9.6 34.1 all-gather.4
  66.8 73.0 all-reduce.3
  147.0 29.1 all-gather.8
  283.4 36.4 reduce-scatter.1
  322.7 42.2 all-reduce.5
  367.1 31.4 all-gather.6
